TPU v7x, 32 devices: a whole 2x2x4 slice. The times are simulated.
32 devices in a mesh: bank: 4 (over y, x), zero: 8 (over z, core).
Axes of the slice: x: 2, y: 2, z: 4, core: 2. Of those that a mesh axis runs over, the one named last changes fastest.
Arguments:
- w_down: float32 [64, 1024, 2048], P('bank', None, 'zero'), may hold values from -0.25 to 0.25
- avg_down: bfloat16 [64, 1024, 2048], P('bank', None, 'zero'), may hold values from -0.09375 to 0.09375
- router_weight: float32 [2048, 64], P('zero', 'bank'), may hold values from -0.125 to 0.125
- router_gain: float32 [2048], P('zero'), may hold values from 0.25 to 1.75
Outputs:
- serve_down: bfloat16 [64, 1024, 2048], P('bank')
- scale_down: float32 [64, 1024], P('bank')
- serve_router: bfloat16 [2048, 64], replicated
All inputs are finite; a program needn't handle non-finite values.
Results may differ from a plain program's by a relative error of at most 0.001.
Values may be sent and summed in bfloat16 or wider, within the bound.
A program may use at most 256 MiB of HBM per device.

v0:
```python
import jax
import jax.numpy as jnp
from jax import lax
from jax.sharding import PartitionSpec as P


def shards(w_down, avg_down, router_weight, router_gain):
    fresh_down = w_down + avg_down.astype(jnp.float32)
    total_down = lax.psum(jnp.sum(fresh_down * fresh_down, axis=2), "zero")
    scale_down = jnp.sqrt(total_down)
    narrow_down = (fresh_down / jnp.expand_dims(scale_down, 2)).astype(jnp.bfloat16)
    serve_down = lax.all_gather(narrow_down, "zero", axis=2, tiled=True)
    part_router = (router_weight * router_gain[:, None]).astype(jnp.bfloat16)
    row_router = lax.all_gather(part_router, "zero", axis=0, tiled=True)
    serve_router = lax.all_gather(row_router, "bank", axis=1, tiled=True)
    return (serve_down, scale_down, serve_router)


def solution(mesh):
    return jax.shard_map(
        shards,
        mesh=mesh,
        in_specs=(P("bank", None, "zero"), P("bank", None, "zero"), P("zero", "bank"), P("zero")),
        out_specs=(P("bank", None, None), P("bank", None), P()),
        check_vma=False,
    )
```

profile of v0, /device:TPU:25, one launch (start us, length us, event | category | flops | bytes accessed | tf_op | source)
XLA Modules:
  0.0 708.1 jit_solution(10193368544461576350)
XLA Ops:
  7.2 0.0 all-reduce.2.cloned.1.call-start
  7.2 9.7 %multiply_reduce_fusion = f32[16,1024]{1,0:T(8,128)} fusion(f32[16,1024,256]{2,1,0:T(8,128)} %param.4, bf16[16,1024,256]{2,1,0:T(8,128)(2,1)} %param.5), kind=kLoop, calls=%fused_computation.1 | loop fusion | flops 16760832 | bytes 25231360 | tf_op jit(solution)/shard_map/reduce_sum | solution.py:9
  17.0 0.0 all-reduce.2.cloned.1.call-update
  17.0 0.0 all-gather.2.cloned.1.call-start
  17.0 53.1 %all-reduce.2.cloned.1.call-done = f32[16,1024]{1,0:T(8,128)} async-done(((f32[16,1024]{1,0:T(8,128)}), f32[16,1024]{1,0:T(8,128)}) %all-reduce.2.cloned.1.call-update) | async-done | bytes 65552 | tf_op jit(solution)/shard_map/psum | solution.py:9
  70.2 0.9 sqrt.3
  71.0 0.0 copy-start
  71.0 0.0 copy-start.1
  71.0 0.0 copy-start.2
  71.1 12.0 %divide_convert_fusion = bf16[16,1024,256]{2,1,0:T(8,128)(2,1)} fusion(f32[16,1024,256]{2,1,0:T(8,128)} %param.4, bf16[16,1024,256]{2,1,0:T(8,128)(2,1)} %param.5, f32[16,1024]{1,0:T(8,128)S(1)} %sqrt.3), kind=kLoop, calls=%fused_computation | loop fusion | flops 16777216 | bytes 33619968 | tf_op jit(solution)/shard_map/convert_element_type | solution.py:11
  83.1 0.0 copy-done
  83.1 0.0 all-gather.2.cloned.1.call-update
  83.1 0.0 copy-done.1
  83.1 0.0 copy-done.2
  83.1 15.2 %all_gather.10 = bf16[2048,16]{0,1:T(8,128)(2,1)S(1)} all-gather(bf16[256,16]{0,1:T(8,128)(2,1)S(1)} %multiply_convert_fusion), channel_id=1, replica_groups=mesh['bank'=4,'zero'=8] {'zero'}, dimensions={0}, use_global_device_ids=true | all-gather | bytes 73728 | tf_op jit(solution)/shard_map/all_gather | solution.py:14
  98.3 7.3 %all_gather.11 = bf16[2048,64]{0,1:T(8,128)(2,1)S(1)} all-gather(bf16[2048,16]{0,1:T(8,128)(2,1)S(1)} %all_gather.10), channel_id=1, replica_groups=mesh['bank'=4,'zero'=8] {'bank'}, dimensions={1}, use_global_device_ids=true | all-gather | bytes 327680 | tf_op jit(solution)/shard_map/all_gather | solution.py:15
  105.7 550.9 %all-gather.2.cloned.1.call-done = bf16[16,1024,2048]{2,1,0:T(8,128)(2,1)} async-done(((bf16[16,1024,256]{2,1,0:T(8,128)(2,1)}), bf16[16,1024,2048]{2,1,0:T(8,128)(2,1)}) %all-gather.2.cloned.1.call-update) | async-done | bytes 67108880 | tf_op jit(solution)/shard_map/all_gather | solution.py:12
  656.6 44.0 %copy.10 = bf16[16,1024,2048]{2,1,0:T(8,128)(2,1)} copy(bf16[16,1024,2048]{2,1,0:T(8,128)(2,1)} %all-gather.2.cloned.1.call-done) | data formatting | bytes 134217728
  700.6 0.7 copy.11
  (1 shorter events, 0.0 us)
Async XLA Ops:
  7.2 63.0 %all-reduce.2.cloned.1.call-start = ((), (), s32[]{:S(2)}) async-start(), calls=%async_computation | async-start | bytes 131072 | tf_op jit(solution)/shard_map/psum | solution.py:9
  17.0 639.6 %all-gather.2.cloned.1.call-start = ((), (), s32[]{:S(2)}) async-start(), calls=%async_computation.1 | async-start | bytes 75497472 | tf_op jit(solution)/shard_map/all_gather | solution.py:12
  71.0 12.1 %copy-start = (f32[16,1024]{1,0:T(8,128)}, f32[16,1024]{1,0:T(8,128)S(1)}, u32[]{:S(2)}) copy-start(f32[16,1024]{1,0:T(8,128)S(1)} %sqrt.3) | copy-start | bytes 196612
  71.0 12.1 %copy-start.1 = (f32[256,16]{0,1:T(8,128)S(1)}, f32[256,16]{0,1:T(8,128)}, u32[]{:S(2)}) copy-start(f32[256,16]{0,1:T(8,128)} %param.6) | copy-start | bytes 49156
  71.0 12.1 %copy-start.2 = (f32[256]{0:T(256)S(1)}, f32[256]{0:T(256)}, u32[]{:S(2)}) copy-start(f32[256]{0:T(256)} %param.7) | copy-start | bytes 3076
Sparse Core Ops, SparseCore 0:
  17.1 53.0 all-reduce.1
  83.2 573.2 all-gather.1
where the time goes:
time: 708 us
  waiting for transfers between devices  604 us (85%)
  local copies, waits for them, and re-layouts  45.6 us (6%)
  blocking collectives  22.5 us (3%)
  other arithmetic  21.8 us (3%)
  between operations  14.1 us (2%)
    all_gather x1, waiting for transfers between devices, shards(): serve_down = lax.all_gather(narrow_down, 'zero', axis=2, tiled=True)  551 us
    psum x1, waiting for transfers between devices, shards(): total_down = lax.psum(jnp.sum(fresh_down * fresh_down, axis=2), 'zero')  53.1 us
    unnamed x8, local copies, waits for them, and re-layouts  44.8 us
    all_gather x1, blocking collectives, shards(): row_router = lax.all_gather(part_router, 'zero', axis=0, tiled=True)  15.2 us
  transfers between devices with their start and end apart: 2, of which 2 were waited for; matrix products, arithmetic and copies ran while one was open for 0% of the time, Pallas kernels for 0%

commit v1 on v0

--- a/solution.py
+++ b/solution.py
@@ -6,7 +6,7 @@
 
 def shards(w_down, avg_down, router_weight, router_gain):
     fresh_down = w_down + avg_down.astype(jnp.float32)
-    total_down = lax.psum(jnp.sum(fresh_down * fresh_down, axis=2), "zero")
+    total_down = jnp.sum(lax.all_gather(jnp.sum(fresh_down * fresh_down, axis=2), "zero"), axis=0)
     scale_down = jnp.sqrt(total_down)
     narrow_down = (fresh_down / jnp.expand_dims(scale_down, 2)).astype(jnp.bfloat16)
     serve_down = lax.all_gather(narrow_down, "zero", axis=2, tiled=True)

time: 708 us -> 668 us (0.944)
  waiting for transfers between devices: 604 us -> 551 us
  blocking collectives: 22.5 us -> 36.7 us
    psum x1 -> x0, waiting for transfers between devices: 53.1 us -> none  [shards(): total_down = lax.psum(jnp.sum(fresh_down * fresh_down, axis=2), 'zero')]
    all_gather x0 -> x1, blocking collectives: none -> 15.4 us  [shards(): lax.all_gather(jnp.sum(fresh_down * fresh_down, axis=2), 'zero')]
  transfers between devices with their start and end apart: 2 -> 1, of which waited for: 2 -> 1; matrix products, arithmetic and copies ran while one was open for 0% -> 0% of each run, Pallas kernels for 0% -> 0%
where the time goes in v1:
time: 668 us
  waiting for transfers between devices  551 us (82%)
  local copies, waits for them, and re-layouts  44.8 us (7%)
  blocking collectives  36.7 us (5%)
  other arithmetic  21.2 us (3%)
  between operations  14.1 us (2%)
    all_gather x1, waiting for transfers between devices, shards(): serve_down = lax.all_gather(narrow_down, 'zero', axis=2, tiled=True)  551 us
    unnamed x8, local copies, waits for them, and re-layouts  44.8 us
    all_gather x1, blocking collectives, shards(): lax.all_gather(jnp.sum(fresh_down * fresh_down, axis=2), 'zero')  15.4 us
    all_gather x1, blocking collectives, shards(): row_router = lax.all_gather(part_router, 'zero', axis=0, tiled=True)  14 us
  transfers between devices with their start and end apart: 1, of which 1 were waited for; matrix products, arithmetic and copies ran while one was open for 0% of the time, Pallas kernels for 0%

profile of v1, /device:TPU:25, one launch (start us, length us, event | category | flops | bytes accessed | tf_op | source)
XLA Modules:
  0.0 667.7 jit_solution(6852669607857805479)
XLA Ops:
  7.2 0.0 all-gather.3.cloned.1.call-start
  7.2 9.1 %multiply_reduce_fusion = f32[16,1024]{1,0:T(8,128)S(1)} fusion(f32[16,1024,256]{2,1,0:T(8,128)} %param.4, bf16[16,1024,256]{2,1,0:T(8,128)(2,1)} %param.5), kind=kLoop, calls=%fused_computation.1 | loop fusion | flops 16760832 | bytes 25231360 | tf_op jit(solution)/shard_map/reduce_sum | solution.py:9
  16.3 15.4 %all-gather = f32[128,1024]{1,0:T(8,128)S(1)} all-gather(f32[16,1024]{1,0:T(8,128)S(1)} %multiply_reduce_fusion), channel_id=2, replica_groups=mesh['bank'=4,'zero'=8] {'zero'}, dimensions={0}, use_global_device_ids=true | all-gather | bytes 589824 | tf_op jit(solution)/shard_map/all_gather | solution.py:9
  31.8 0.0 copy-start
  31.8 0.0 copy-start.1
  31.8 0.0 copy-start.2
  31.8 12.0 %divide_convert_fusion = bf16[16,1024,256]{2,1,0:T(8,128)(2,1)} fusion(f32[16,1024,256]{2,1,0:T(8,128)} %param.4, bf16[16,1024,256]{2,1,0:T(8,128)(2,1)} %param.5, f32[16,1024]{1,0:T(8,128)S(1)} %sqrt.7), kind=kLoop, calls=%fused_computation | loop fusion | flops 16777216 | bytes 33619968 | tf_op jit(solution)/shard_map/convert_element_type | solution.py:11
  43.8 0.0 copy-done
  43.8 0.0 all-gather.3.cloned.1.call-update
  43.9 0.0 copy-done.1
  43.9 0.0 copy-done.2
  43.9 14.0 %all_gather.18 = bf16[2048,16]{0,1:T(8,128)(2,1)S(1)} all-gather(bf16[256,16]{0,1:T(8,128)(2,1)S(1)} %multiply_convert_fusion), channel_id=1, replica_groups=mesh['bank'=4,'zero'=8] {'zero'}, dimensions={0}, use_global_device_ids=true | all-gather | bytes 73728 | tf_op jit(solution)/shard_map/all_gather | solution.py:14
  57.9 7.4 %all_gather.19 = bf16[2048,64]{0,1:T(8,128)(2,1)S(1)} all-gather(bf16[2048,16]{0,1:T(8,128)(2,1)S(1)} %all_gather.18), channel_id=1, replica_groups=mesh['bank'=4,'zero'=8] {'bank'}, dimensions={1}, use_global_device_ids=true | all-gather | bytes 327680 | tf_op jit(solution)/shard_map/all_gather | solution.py:15
  65.2 550.8 %all-gather.3.cloned.1.call-done = bf16[16,1024,2048]{2,1,0:T(8,128)(2,1)} async-done(((bf16[16,1024,256]{2,1,0:T(8,128)(2,1)}), bf16[16,1024,2048]{2,1,0:T(8,128)(2,1)}) %all-gather.3.cloned.1.call-update) | async-done | bytes 67108880 | tf_op jit(solution)/shard_map/all_gather | solution.py:12
  616.1 44.0 %copy.9 = bf16[16,1024,2048]{2,1,0:T(8,128)(2,1)} copy(bf16[16,1024,2048]{2,1,0:T(8,128)(2,1)} %all-gather.3.cloned.1.call-done) | data formatting | bytes 134217728
  660.1 0.7 copy.10
  (3 shorter events, 0.1 us)
Async XLA Ops:
  7.2 608.9 %all-gather.3.cloned.1.call-start = ((), (), s32[]{:S(2)}) async-start(), calls=%async_computation | async-start | bytes 75497472 | tf_op jit(solution)/shard_map/all_gather | solution.py:12
  31.8 12.1 %copy-start = (f32[16,1024]{1,0:T(8,128)}, f32[16,1024]{1,0:T(8,128)S(1)}, u32[]{:S(2)}) copy-start(f32[16,1024]{1,0:T(8,128)S(1)} %sqrt.7) | copy-start | bytes 196612
  31.8 12.1 %copy-start.1 = (f32[256,16]{0,1:T(8,128)S(1)}, f32[256,16]{0,1:T(8,128)}, u32[]{:S(2)}) copy-start(f32[256,16]{0,1:T(8,128)} %param.6) | copy-start | bytes 49156
  31.8 12.1 %copy-start.2 = (f32[256]{0:T(256)S(1)}, f32[256]{0:T(256)}, u32[]{:S(2)}) copy-start(f32[256]{0:T(256)} %param.7) | copy-start | bytes 3076
Sparse Core Ops, SparseCore 0:
  44.0 572.0 all-gather.2

commit v2 on v0

--- a/solution.py
+++ b/solution.py
@@ -9,7 +9,7 @@
     total_down = lax.psum(jnp.sum(fresh_down * fresh_down, axis=2), "zero")
     scale_down = jnp.sqrt(total_down)
     narrow_down = (fresh_down / jnp.expand_dims(scale_down, 2)).astype(jnp.bfloat16)
-    serve_down = lax.all_gather(narrow_down, "zero", axis=2, tiled=True)
+    serve_down = jnp.concatenate(lax.all_gather(narrow_down, "zero"), axis=2)
     part_router = (router_weight * router_gain[:, None]).astype(jnp.bfloat16)
     row_router = lax.all_gather(part_router, "zero", axis=0, tiled=True)
     serve_router = lax.all_gather(row_router, "bank", axis=1, tiled=True)

time: 708 us -> 703 us (level)
  waiting for transfers between devices: 604 us -> 594 us
    reshape x0 -> x1, local copies, waits for them, and re-layouts: none -> 44.3 us  [shards(): serve_down = jnp.concatenate(lax.all_gather(narrow_down, 'zero'), axis=2)]
    unnamed x8 -> x7, local copies, waits for them, and re-layouts: 44.8 us -> 0.72 us
    all_gather x1, waiting for transfers between devices: 551 us -> 541 us  [shards(): serve_down = jnp.concatenate(lax.all_gather(narrow_down, 'zero'), axis=2)]
where the time goes in v2:
time: 703 us; the launch traced here: 698 us
  waiting for transfers between devices  594 us (84%)
  local copies, waits for them, and re-layouts  45.9 us (7%)
  blocking collectives  22.5 us (3%)
  other arithmetic  21.8 us (3%)
  between operations  14.1 us (2%)
    all_gather x1, waiting for transfers between devices, shards(): serve_down = jnp.concatenate(lax.all_gather(narrow_down, 'zero'), axis=2)  541 us
    psum x1, waiting for transfers between devices, shards(): total_down = lax.psum(jnp.sum(fresh_down * fresh_down, axis=2), 'zero')  53.1 us
    reshape x1, local copies, waits for them, and re-layouts, shards(): serve_down = jnp.concatenate(lax.all_gather(narrow_down, 'zero'), axis=2)  44.3 us
    all_gather x1, blocking collectives, shards(): row_router = lax.all_gather(part_router, 'zero', axis=0, tiled=True)  15.2 us
  transfers between devices with their start and end apart: 2, of which 2 were waited for; matrix products, arithmetic and copies ran while one was open for 0% of the time, Pallas kernels for 0%

profile of v2, /device:TPU:25, one launch (start us, length us, event | category | flops | bytes accessed | tf_op | source)
XLA Modules:
  0.0 698.2 jit_solution(3893677561080732542)
XLA Ops:
  7.2 0.0 all-reduce.2.cloned.1.call-start
  7.2 9.7 %multiply_reduce_fusion = f32[16,1024]{1,0:T(8,128)} fusion(f32[16,1024,256]{2,1,0:T(8,128)} %param.4, bf16[16,1024,256]{2,1,0:T(8,128)(2,1)} %param.5), kind=kLoop, calls=%fused_computation.1 | loop fusion | flops 16760832 | bytes 25231360 | tf_op jit(solution)/shard_map/reduce_sum | solution.py:9
  17.0 0.0 all-reduce.2.cloned.1.call-update
  17.0 0.0 all-gather.3.cloned.1.call-start
  17.0 53.1 %all-reduce.2.cloned.1.call-done = f32[16,1024]{1,0:T(8,128)} async-done(((f32[16,1024]{1,0:T(8,128)}), f32[16,1024]{1,0:T(8,128)}) %all-reduce.2.cloned.1.call-update) | async-done | bytes 65552 | tf_op jit(solution)/shard_map/psum | solution.py:9
  70.2 0.9 sqrt.3
  71.0 0.0 copy-start
  71.0 0.0 copy-start.1
  71.0 0.0 copy-start.2
  71.1 12.0 %divide_convert_fusion = bf16[16,1024,256]{2,1,0:T(8,128)(2,1)} fusion(f32[16,1024,256]{2,1,0:T(8,128)} %param.4, bf16[16,1024,256]{2,1,0:T(8,128)(2,1)} %param.5, f32[16,1024]{1,0:T(8,128)S(1)} %sqrt.3), kind=kLoop, calls=%fused_computation | loop fusion | flops 16777216 | bytes 33619968 | tf_op jit(solution)/shard_map/convert_element_type | solution.py:11
  83.1 0.0 copy-done
  83.1 0.0 all-gather.3.cloned.1.call-update
  83.1 0.0 copy-done.1
  83.1 0.0 copy-done.2
  83.1 15.2 %all_gather.14 = bf16[2048,16]{0,1:T(8,128)(2,1)S(1)} all-gather(bf16[256,16]{0,1:T(8,128)(2,1)S(1)} %multiply_convert_fusion), channel_id=1, replica_groups=mesh['bank'=4,'zero'=8] {'zero'}, dimensions={0}, use_global_device_ids=true | all-gather | bytes 73728 | tf_op jit(solution)/shard_map/all_gather | solution.py:14
  98.3 7.3 %all_gather.15 = bf16[2048,64]{0,1:T(8,128)(2,1)S(1)} all-gather(bf16[2048,16]{0,1:T(8,128)(2,1)S(1)} %all_gather.14), channel_id=1, replica_groups=mesh['bank'=4,'zero'=8] {'bank'}, dimensions={1}, use_global_device_ids=true | all-gather | bytes 327680 | tf_op jit(solution)/shard_map/all_gather | solution.py:15
  105.7 540.6 %all-gather.3.cloned.1.call-done = bf16[128,1024,256]{2,1,0:T(8,128)(2,1)} async-done(((bf16[16,1024,256]{2,1,0:T(8,128)(2,1)}), bf16[128,1024,256]{2,1,0:T(8,128)(2,1)}) %all-gather.3.cloned.1.call-update) | async-done | bytes 67108880 | tf_op jit(solution)/shard_map/all_gather | solution.py:12
  646.3 44.3 %copy.9 = bf16[8,16,128,8,256]{4,3,0,2,1:T(8,128)(2,1)} copy(bf16[8,16,128,8,256]{4,3,2,1,0:T(8,128)(2,1)} %bitcast.3) | data formatting | bytes 134217728 | tf_op jit(solution)/shard_map/reshape | solution.py:12
  690.6 0.7 copy.12
  (1 shorter events, 0.0 us)
Async XLA Ops:
  7.2 63.0 %all-reduce.2.cloned.1.call-start = ((), (), s32[]{:S(2)}) async-start(), calls=%async_computation | async-start | bytes 131072 | tf_op jit(solution)/shard_map/psum | solution.py:9
  17.0 629.3 %all-gather.3.cloned.1.call-start = ((), (), s32[]{:S(2)}) async-start(), calls=%async_computation.1 | async-start | bytes 75497472 | tf_op jit(solution)/shard_map/all_gather | solution.py:12
  71.0 12.1 %copy-start = (f32[16,1024]{1,0:T(8,128)}, f32[16,1024]{1,0:T(8,128)S(1)}, u32[]{:S(2)}) copy-start(f32[16,1024]{1,0:T(8,128)S(1)} %sqrt.3) | copy-start | bytes 196612
  71.0 12.1 %copy-start.1 = (f32[256,16]{0,1:T(8,128)S(1)}, f32[256,16]{0,1:T(8,128)}, u32[]{:S(2)}) copy-start(f32[256,16]{0,1:T(8,128)} %param.6) | copy-start | bytes 49156
  71.0 12.1 %copy-start.2 = (f32[256]{0:T(256)S(1)}, f32[256]{0:T(256)}, u32[]{:S(2)}) copy-start(f32[256]{0:T(256)} %param.7) | copy-start | bytes 3076
Sparse Core Ops, SparseCore 0:
  17.1 53.0 all-reduce.1
  83.2 563.0 all-gather.2
